TPU v7x, 32 devices: a whole 2x2x4 slice. The times are simulated.
32 devices in a mesh: kpt: 2 (over y), ga: 16 (over z, x, core).
Axes of the slice: x: 2, y: 2, z: 4, core: 2. Of those that a mesh axis runs over, the one named last changes fastest.
Arguments:
- miller_index: int32 [3, 12288], P(None, 'ga'), may hold values from -12 to 12
- kpoint: float32 [6], P('kpt'), parts along dimension 0, may hold values from -0.5 to 0.5
- waves: bfloat16 [2, 256, 12288], P(None, 'kpt', 'ga'), parts along dimension 1, may hold values from -6 to 6
- species: int32 [16], replicated, may hold values from 0 to 3
- counts: int32 [16], replicated, may hold values from 1 to 8
- positions: int32 [3, 16], replicated, may hold values from 0 to 63
- radial_coef: float32 [4, 8, 16], replicated, may hold values from -4 to 4
- coupling: float32 [16, 8, 8], replicated, as said below
Outputs:
- applied: bfloat16 [2, 256, 12288], P(None, 'kpt', 'ga'), parts along dimension 1
- energy: float32 [256], P('kpt'), parts along dimension 0
There are 2 independent parts, one for each index of `kpt`. A program takes and returns all parts, laid end to end along the dimension named above; an argument that names none is the same for every part. Nothing has to cross between parts.
Inputs may be any that keep to these rules, and one draw needn't show every extreme that they name: `coupling`: symmetric in its last two dimensions.
All inputs are finite; a program needn't handle non-finite values.
Results may differ from a plain program's by a relative error of at most 0.0062.
Values may be sent and summed in bfloat16 or wider, within the bound.
A program may use at most 64 MiB of HBM per device.

v0:
```python
import math
import jax
import jax.numpy as jnp
from jax import lax
from jax.sharding import PartitionSpec as P

PROJ = 8
MGRID = 64
ATOM_BLOCK = 16


def prepare(miller_index, kpoint, terms):
    shifted = miller_index.astype(jnp.float32) + kpoint[:, None]
    squared = jnp.sum(shifted * shifted, axis=0)
    widths = 0.001 * 1.5 ** jnp.arange(terms).astype(jnp.float32)
    basis = jnp.exp(-widths[:, None] * squared[None, :])
    angular = jnp.concatenate(
        [jnp.ones_like(squared)[None], shifted / jnp.sqrt(squared + 1.0)[None]], 0
    )
    angular = jnp.concatenate([angular, angular], 0)
    return (basis, angular)


def projectors(
    first, miller_index, kpoint, basis, angular, species, counts, positions, radial_coef, scaling
):
    kinds = lax.dynamic_slice_in_dim(species, first, ATOM_BLOCK)
    numbers = lax.dynamic_slice_in_dim(counts, first, ATOM_BLOCK)
    places = lax.dynamic_slice_in_dim(positions, first, ATOM_BLOCK, 1)
    selector = (kinds[:, None] == jnp.arange(radial_coef.shape[0])[None, :]).astype(jnp.float32)
    chosen = jnp.einsum("as,sjr->ajr", selector, radial_coef, precision=lax.Precision.HIGHEST)
    radial = jnp.einsum("ajr,rg->ajg", chosen, basis, precision=lax.Precision.HIGHEST)
    active = (jnp.arange(PROJ)[None, :] < numbers[:, None]).astype(jnp.float32)
    amplitude = radial * angular[None] * active[:, :, None] * scaling
    winding = jnp.mod(jnp.sum(miller_index[:, None, :] * places[:, :, None], axis=0), MGRID)
    offset = jnp.sum(kpoint[:, None] * places.astype(jnp.float32), axis=0)
    phase = 2.0 * math.pi / MGRID * (winding.astype(jnp.float32) + offset[:, None])
    planes = miller_index.shape[1]
    real_part = (
        (amplitude * jnp.cos(phase)[:, None, :])
        .astype(jnp.bfloat16)
        .reshape(ATOM_BLOCK * PROJ, planes)
    )
    imag_part = (
        (-amplitude * jnp.sin(phase)[:, None, :])
        .astype(jnp.bfloat16)
        .reshape(ATOM_BLOCK * PROJ, planes)
    )
    return (real_part, imag_part)


def measure(real_part, imag_part, coeffs):
    over_re = jnp.einsum(
        "sg,bg->sb", real_part, coeffs[0], preferred_element_type=jnp.float32
    ) + jnp.einsum("sg,bg->sb", imag_part, coeffs[1], preferred_element_type=jnp.float32)
    over_im = jnp.einsum(
        "sg,bg->sb", real_part, coeffs[1], preferred_element_type=jnp.float32
    ) - jnp.einsum("sg,bg->sb", imag_part, coeffs[0], preferred_element_type=jnp.float32)
    return jnp.stack([over_re, over_im])


def spread(rows, real_part, imag_part):
    out_re = jnp.einsum(
        "sb,sg->bg", rows[0], real_part, preferred_element_type=jnp.float32
    ) - jnp.einsum("sb,sg->bg", rows[1], imag_part, preferred_element_type=jnp.float32)
    out_im = jnp.einsum(
        "sb,sg->bg", rows[1], real_part, preferred_element_type=jnp.float32
    ) + jnp.einsum("sb,sg->bg", rows[0], imag_part, preferred_element_type=jnp.float32)
    return jnp.stack([out_re, out_im])


def on_device(miller_index, kpoint, waves, species, counts, positions, radial_coef, coupling):
    planes = waves.shape[2]
    bands = waves.shape[1]
    scaling = 1.0 / math.sqrt(planes * lax.axis_size("ga"))
    atoms = coupling.shape[0]
    slots_all = atoms * PROJ
    blocks = atoms // ATOM_BLOCK
    width = ATOM_BLOCK * PROJ
    basis, angular = prepare(miller_index, kpoint, radial_coef.shape[2])

    def build(index):
        return projectors(
            index * ATOM_BLOCK,
            miller_index,
            kpoint,
            basis,
            angular,
            species,
            counts,
            positions,
            radial_coef,
            scaling,
        )

    empty = jnp.zeros((2, bands, planes), jnp.float32)

    def first_pass(index, table):
        real_part, imag_part = build(index)
        return lax.dynamic_update_slice_in_dim(
            table, measure(real_part, imag_part, waves), index * width, 1
        )

    local = lax.fori_loop(0, blocks, first_pass, jnp.zeros((2, slots_all, bands), jnp.float32))
    summed = lax.psum(local, "ga")
    shaped = summed.reshape(2, atoms, PROJ, summed.shape[2])
    weighted = jnp.einsum("aij,cajb->caib", coupling, shaped, precision=lax.Precision.HIGHEST)
    weighted = weighted.reshape(2, atoms * PROJ, summed.shape[2])
    energy = jnp.sum(summed * weighted, axis=(0, 1))
    table = weighted.astype(jnp.bfloat16)

    def second_pass(index, output):
        real_part, imag_part = build(index)
        rows = lax.dynamic_slice_in_dim(table, index * width, width, 1)
        return output + spread(rows, real_part, imag_part)

    output = lax.fori_loop(0, blocks, second_pass, empty)
    return (output.astype(jnp.bfloat16), energy / slots_all)


def solution(mesh):
    in_specs = (P(None, "ga"), P("kpt"), P(None, "kpt", "ga"), P(), P(), P(), P(), P())
    out_specs = (P(None, "kpt", "ga"), P("kpt"))
    return jax.shard_map(
        on_device, mesh=mesh, in_specs=in_specs, out_specs=out_specs, check_vma=False
    )
```

profile of v0, /device:TPU:8, one launch (start us, length us, event | category | flops | bytes accessed | tf_op | source)
XLA Modules:
  0.0 116.9 jit_solution(3049479459820801523)
XLA Ops:
  7.3 0.6 copy-done.6
  7.8 0.8 multiply_reduce_fusion.2
  8.6 0.8 multiply_reduce_fusion.1
  9.6 0.6 copy-done.8
  10.3 0.3 fusion.40
  10.6 0.4 copy-done.7
  10.9 0.2 fusion.33
  11.2 0.6 fusion.8
  11.8 0.4 copy-done.1
  12.2 0.2 fusion.9
  12.4 0.2 fusion.13
  12.6 0.2 fusion.5
  12.8 0.2 fusion.6
  13.1 0.7 pad_maximum_fusion.1
  13.8 0.7 copy-done.4
  14.6 91.3 %all-reduce.2.cloned.1.call-done = f32[2,128,128]{2,1,0:T(8,128)} async-done(((f32[2,128,128]{2,1,0:T(8,128)}), f32[2,128,128]{2,1,0:T(8,128)}) %all-reduce.2.cloned.1.call-update) | async-done | bytes 131088 | tf_op jit(solution)/shard_map/psum | solution.py:105
  105.9 1.1 convolution_bitcast_fusion
  107.1 0.2 fusion.30
  107.3 0.2 fusion.29
  107.6 0.7 copy-done.2
  108.3 0.5 broadcast_multiply_fusion
  108.8 0.2 fusion.3
  109.1 0.2 fusion.4
  109.3 0.8 pad_maximum_fusion
  (24 shorter events, 0.5 us)
Async XLA Ops:
  7.2 3.4 %copy-start = (f32[4,8,16]{2,1,0:T(8,128)S(1)}, f32[4,8,16]{2,1,0:T(8,128)}, u32[]{:S(2)}) copy-start(f32[4,8,16]{2,1,0:T(8,128)} %param.14) | copy-start | bytes 6148
  7.2 0.7 copy-start.6
  7.2 2.2 %copy-start.3 = (s32[3,768]{1,0:T(4,128)S(1)}, s32[3,768]{1,0:T(4,128)}, u32[]{:S(2)}) copy-start(s32[3,768]{1,0:T(4,128)} %param.8) | copy-start | bytes 27652
  7.2 98.7 %all-reduce.2.cloned.1.call-start = ((), (), s32[]{:S(2)}) async-start(), calls=%async_computation | async-start | bytes 262144 | tf_op jit(solution)/shard_map/psum | solution.py:105
  8.6 0.8 copy-start.5
  9.5 0.7 copy-start.8
  10.3 0.7 copy-start.7
  11.2 1.0 copy-start.1
  13.7 0.8 copy-start.4
  107.3 0.9 copy-start.2
Sparse Core Ops, SparseCore 0:
  13.9 92.0 all-reduce.1
where the time goes:
time: 117 us
  waiting for transfers between devices  91.4 us (78%)
  between operations  14.2 us (12%)
  other arithmetic  4.1 us (4%)
  matrix products  3.75 us (3%)
  local copies, waits for them, and re-layouts  3.45 us (3%)
    psum x1, waiting for transfers between devices, on_device(): summed = lax.psum(local, 'ga')  91.3 us
    unnamed x19, local copies, waits for them, and re-layouts  3.43 us
  transfers between devices with their start and end apart: 1, of which 1 were waited for; matrix products, arithmetic and copies ran while one was open for 0% of the time, Pallas kernels for 0%

commit v1 on v0

--- a/solution.py
+++ b/solution.py
@@ -102,7 +102,9 @@
         )
 
     local = lax.fori_loop(0, blocks, first_pass, jnp.zeros((2, slots_all, bands), jnp.float32))
-    summed = lax.psum(local, "ga")
+    summed = local
+    for hop in (1, 2, 4, 8):
+        summed = summed + lax.ppermute(summed, "ga", [(dev, dev ^ hop) for dev in range(16)])
     shaped = summed.reshape(2, atoms, PROJ, summed.shape[2])
     weighted = jnp.einsum("aij,cajb->caib", coupling, shaped, precision=lax.Precision.HIGHEST)
     weighted = weighted.reshape(2, atoms * PROJ, summed.shape[2])

time: 117 us -> 30.7 us (0.26)
  the two profiles are of different devices: /device:TPU:8 before, /device:TPU:0 now
where the time goes in v1:
time: 30.7 us; the launch traced here: 30.4 us
  waiting for transfers between devices  12.9 us (42%)
  starting transfers between devices  8.24 us (27%)
  other arithmetic  3.51 us (11%)
  matrix products  2.85 us (9%)
  local copies, waits for them, and re-layouts  2.1 us (7%)
  between operations  0.86 us (3%)
    ppermute x4, waiting for transfers between devices, on_device(): lax.ppermute(summed, 'ga', [(dev, dev ^ hop) for dev in range(16)])  12.9 us
    ppermute x4, starting transfers between devices, on_device(): lax.ppermute(summed, 'ga', [(dev, dev ^ hop) for dev in range(16)])  8.24 us
    unnamed x17, local copies, waits for them, and re-layouts  2.09 us
    reduce_sum x1, other arithmetic, prepare(): squared = jnp.sum(shifted * shifted, axis=0)  0.8 us
    another operation x1, other arithmetic, spread(): return jnp.stack([out_re, out_im])  0.78 us
    reduce_sum x1, other arithmetic, projectors(): offset = jnp.sum(kpoint[:, None] * places.astype(jnp.float32), axis=0)  0.77 us
  transfers between devices with their start and end apart: 4, of which 4 were waited for; matrix products, arithmetic and copies ran while one was open for 0% of the time, Pallas kernels for 0%

profile of v1, /device:TPU:0, one launch (start us, length us, event | category | flops | bytes accessed | tf_op | source)
XLA Modules:
  0.0 30.4 jit_solution(6824349105550514421)
XLA Ops:
  0.7 0.6 %copy-done.5 = f32[3]{0:T(128)S(1)} copy-done((f32[3]{0:T(128)S(1)}, f32[3]{0:T(128)}, u32[]{:S(2)}) %copy-start.5) | copy-done | bytes 36
  1.3 0.8 %multiply_reduce_fusion.2 = f32[16]{0:T(128)S(1)} fusion(s32[3,16]{1,0:T(4,128)} %param.13, f32[3]{0:T(128)S(1)} %copy-done.5), kind=kLoop, calls=%fused_computation.64 | loop fusion | flops 128 | bytes 268 | tf_op jit(solution)/shard_map/while/body/eval_jaxpr/reduce_sum | solution.py:36
  2.1 0.8 %multiply_reduce_fusion.1 = f32[768]{0:T(1024)S(1)} fusion(s32[3,768]{1,0:T(4,128)} %param.8, f32[3]{0:T(128)S(1)} %copy-done.5), kind=kLoop, calls=%fused_computation.55 | loop fusion | flops 8448 | bytes 12300 | tf_op jit(solution)/shard_map/reduce_sum | solution.py:14
  3.1 0.6 %copy-done.7 = s32[16]{0:T(128)S(1)} copy-done((s32[16]{0:T(128)S(1)}, s32[16]{0:T(128)}, u32[]{:S(2)}) %copy-start.7) | copy-done | bytes 88
  3.8 0.3 fusion.40
  4.0 0.4 %copy-done.6 = s32[16]{0:T(128)S(1)} copy-done((s32[16]{0:T(128)S(1)}, s32[16]{0:T(128)}, u32[]{:S(2)}) %copy-start.6) | copy-done | bytes 88
  4.7 0.6 %fusion.8 = (bf16[128,768]{1,0:T(8,128)(2,1)S(1)}, bf16[128,768]{1,0:T(8,128)(2,1)S(1)}) fusion(f32[16,768]{1,0:T(8,128)S(1)} %get-tuple-element.52, f32[16,768]{1,0:T(8,128)S(1)} %get-tuple-element.53, f32[16,8]{1,0:T(8,128)S(1)} %fusion.38, f32[8,768]{1,0:T(8,128)S(1)} %pad_maximum_fusion.2, f32[768]{0:T(1024)S(1)} %multiply_reduce_fusion.1, ...), kind=kOutput, calls=%fused_computation.17 | convolution fusion | flops 19673088 | bytes 527936 | tf_op jit(solution)/shard_map/while/body/eval_jaxpr/ajr,rg->ajg/dot_general | solution.py:32
  5.2 0.4 %copy-done.1 = bf16[2,128,768]{2,1,0:T(8,128)(2,1)S(1)} copy-done((bf16[2,128,768]{2,1,0:T(8,128)(2,1)S(1)}, bf16[2,128,768]{2,1,0:T(8,128)(2,1)}, u32[]{:S(2)}) %copy-start.1) | copy-done | bytes 393240
  6.3 0.2 fusion.6
  6.5 0.6 %collective-permute-start = (f32[2,128,128]{2,1,0:T(8,128)S(1)}, f32[2,128,128]{2,1,0:T(8,128)S(1)}, u32[]{:S(2)}, u32[]{:S(2)}) collective-permute-start(f32[2,128,128]{2,1,0:T(8,128)S(1)} %pad_maximum_fusion.1), channel_id=1, source_target_pairs={{0,1},{1,0},{2,3},{3,2},{4,5},{5,4},{6,7},{7,6},{8,9},{9,8},{10,11... | collective-permute-start | bytes 393224 | tf_op jit(solution)/shard_map/ppermute | solution.py:107
  7.1 1.0 %collective-permute-done = f32[2,128,128]{2,1,0:T(8,128)S(1)} collective-permute-done((f32[2,128,128]{2,1,0:T(8,128)S(1)}, f32[2,128,128]{2,1,0:T(8,128)S(1)}, u32[]{:S(2)}, u32[]{:S(2)}) %collective-permute-start) | collective-permute-done | bytes 131104 | tf_op jit(solution)/shard_map/ppermute | solution.py:107
  8.1 2.9 %collective-permute-start.1 = (f32[2,128,128]{2,1,0:T(8,128)S(1)}, f32[2,128,128]{2,1,0:T(8,128)S(1)}, u32[]{:S(2)}, u32[]{:S(2)}) collective-permute-start(f32[2,128,128]{2,1,0:T(8,128)S(1)} %fusion.41), channel_id=1, source_target_pairs={{0,2},{1,3},{2,0},{3,1},{4,6},{5,7},{6,4},{7,5},{8,10},{9,11},{10,... | collective-permute-start | bytes 393224 | tf_op jit(solution)/shard_map/ppermute | solution.py:107
  11.0 3.8 %collective-permute-done.1 = f32[2,128,128]{2,1,0:T(8,128)S(1)} collective-permute-done((f32[2,128,128]{2,1,0:T(8,128)S(1)}, f32[2,128,128]{2,1,0:T(8,128)S(1)}, u32[]{:S(2)}, u32[]{:S(2)}) %collective-permute-start.1) | collective-permute-done | bytes 131104 | tf_op jit(solution)/shard_map/ppermute | solution.py:107
  14.9 1.9 %collective-permute-start.2 = (f32[2,128,128]{2,1,0:T(8,128)S(1)}, f32[2,128,128]{2,1,0:T(8,128)S(1)}, u32[]{:S(2)}, u32[]{:S(2)}) collective-permute-start(f32[2,128,128]{2,1,0:T(8,128)S(1)} %fusion.55), channel_id=1, source_target_pairs={{0,4},{1,5},{2,6},{3,7},{4,0},{5,1},{6,2},{7,3},{8,12},{9,13},{10,... | collective-permute-start | bytes 393224 | tf_op jit(solution)/shard_map/ppermute | solution.py:107
  16.8 3.2 %collective-permute-done.2 = f32[2,128,128]{2,1,0:T(8,128)S(1)} collective-permute-done((f32[2,128,128]{2,1,0:T(8,128)S(1)}, f32[2,128,128]{2,1,0:T(8,128)S(1)}, u32[]{:S(2)}, u32[]{:S(2)}) %collective-permute-start.2) | collective-permute-done | bytes 131104 | tf_op jit(solution)/shard_map/ppermute | solution.py:107
  19.9 2.9 %collective-permute-start.3 = (f32[2,128,128]{2,1,0:T(8,128)S(1)}, f32[2,128,128]{2,1,0:T(8,128)S(1)}, u32[]{:S(2)}, u32[]{:S(2)}) collective-permute-start(f32[2,128,128]{2,1,0:T(8,128)S(1)} %add.111), channel_id=1, source_target_pairs={{0,8},{1,9},{2,10},{3,11},{4,12},{5,13},{6,14},{7,15},{8,0},{9,1},... | collective-permute-start | bytes 393224 | tf_op jit(solution)/shard_map/ppermute | solution.py:107
  22.9 4.9 %collective-permute-done.3 = f32[2,128,128]{2,1,0:T(8,128)S(1)} collective-permute-done((f32[2,128,128]{2,1,0:T(8,128)S(1)}, f32[2,128,128]{2,1,0:T(8,128)S(1)}, u32[]{:S(2)}, u32[]{:S(2)}) %collective-permute-start.3) | collective-permute-done | bytes 131104 | tf_op jit(solution)/shard_map/ppermute | solution.py:107
  27.8 0.2 convolution_bitcast_fusion
  28.2 0.2 fusion.30
  28.4 0.2 fusion.29
  28.6 0.5 %broadcast_multiply_fusion = f32[128]{0:T(128)} fusion(f32[128]{0:T(128)S(1)} %fusion.19), kind=kLoop, calls=%fused_computation.66 | loop fusion | flops 128 | bytes 1024 | tf_op jit(solution)/shard_map/div | solution.py:120
  29.2 0.2 fusion.3
  29.4 0.2 fusion.4
  29.6 0.8 %pad_maximum_fusion = bf16[2,128,768]{2,1,0:T(8,128)(2,1)} fusion(bf16[1,128,768]{2,1,0:T(8,128)(2,1)S(1)} %fusion.3, bf16[1,128,768]{2,1,0:T(8,128)(2,1)S(1)} %fusion.4), kind=kLoop, calls=%fused_computation.13 | loop fusion | flops 196608 | bytes 786432 | tf_op jit(solution)/shard_map/while/body/eval_jaxpr/stack | solution.py:69
  (31 shorter events, 1.4 us)
Async XLA Ops:
  0.6 3.4 %copy-start = (f32[4,8,16]{2,1,0:T(8,128)S(1)}, f32[4,8,16]{2,1,0:T(8,128)}, u32[]{:S(2)}) copy-start(f32[4,8,16]{2,1,0:T(8,128)} %param.14) | copy-start | bytes 6148
  0.6 0.7 %copy-start.5 = (f32[3]{0:T(128)S(1)}, f32[3]{0:T(128)}, u32[]{:S(2)}) copy-start(f32[3]{0:T(128)} %param.9) | copy-start | bytes 40
  0.7 2.2 %copy-start.2 = (s32[3,768]{1,0:T(4,128)S(1)}, s32[3,768]{1,0:T(4,128)}, u32[]{:S(2)}) copy-start(s32[3,768]{1,0:T(4,128)} %param.8) | copy-start | bytes 27652
  2.1 0.8 %copy-start.4 = (s32[3,16]{1,0:T(4,128)S(1)}, s32[3,16]{1,0:T(4,128)}, u32[]{:S(2)}) copy-start(s32[3,16]{1,0:T(4,128)} %param.13) | copy-start | bytes 580
  3.0 0.7 %copy-start.7 = (s32[16]{0:T(128)S(1)}, s32[16]{0:T(128)}, u32[]{:S(2)}) copy-start(s32[16]{0:T(128)} %param.12) | copy-start | bytes 196
  3.8 0.7 %copy-start.6 = (s32[16]{0:T(128)S(1)}, s32[16]{0:T(128)}, u32[]{:S(2)}) copy-start(s32[16]{0:T(128)} %param.11) | copy-start | bytes 196
  4.6 1.0 %copy-start.1 = (bf16[2,128,768]{2,1,0:T(8,128)(2,1)S(1)}, bf16[2,128,768]{2,1,0:T(8,128)(2,1)}, u32[]{:S(2)}) copy-start(bf16[2,128,768]{2,1,0:T(8,128)(2,1)} %param.10) | copy-start | bytes 1179652
  6.5 1.5 %collective-permute-start = (f32[2,128,128]{2,1,0:T(8,128)S(1)}, f32[2,128,128]{2,1,0:T(8,128)S(1)}, u32[]{:S(2)}, u32[]{:S(2)}) collective-permute-start(f32[2,128,128]{2,1,0:T(8,128)S(1)} %pad_maximum_fusion.1), channel_id=1, source_target_pairs={{0,1},{1,0},{2,3},{3,2},{4,5},{5,4},{6,7},{7,6},{8,9},{9,8},{10,11... | collective-permute-start | bytes 393224 | tf_op jit(solution)/shard_map/ppermute | solution.py:107
  8.1 6.7 %collective-permute-start.1 = (f32[2,128,128]{2,1,0:T(8,128)S(1)}, f32[2,128,128]{2,1,0:T(8,128)S(1)}, u32[]{:S(2)}, u32[]{:S(2)}) collective-permute-start(f32[2,128,128]{2,1,0:T(8,128)S(1)} %fusion.41), channel_id=1, source_target_pairs={{0,2},{1,3},{2,0},{3,1},{4,6},{5,7},{6,4},{7,5},{8,10},{9,11},{10,... | collective-permute-start | bytes 393224 | tf_op jit(solution)/shard_map/ppermute | solution.py:107
  14.9 8.0 %copy-start.3 = (f32[16,8,8]{0,2,1:T(8,128)S(1)}, f32[16,8,8]{0,2,1:T(8,128)}, u32[]{:S(2)}) copy-start(f32[16,8,8]{0,2,1:T(8,128)} %param.15) | copy-start | bytes 12292
  14.9 5.0 %collective-permute-start.2 = (f32[2,128,128]{2,1,0:T(8,128)S(1)}, f32[2,128,128]{2,1,0:T(8,128)S(1)}, u32[]{:S(2)}, u32[]{:S(2)}) collective-permute-start(f32[2,128,128]{2,1,0:T(8,128)S(1)} %fusion.55), channel_id=1, source_target_pairs={{0,4},{1,5},{2,6},{3,7},{4,0},{5,1},{6,2},{7,3},{8,12},{9,13},{10,... | collective-permute-start | bytes 393224 | tf_op jit(solution)/shard_map/ppermute | solution.py:107
  19.9 7.9 %collective-permute-start.3 = (f32[2,128,128]{2,1,0:T(8,128)S(1)}, f32[2,128,128]{2,1,0:T(8,128)S(1)}, u32[]{:S(2)}, u32[]{:S(2)}) collective-permute-start(f32[2,128,128]{2,1,0:T(8,128)S(1)} %add.111), channel_id=1, source_target_pairs={{0,8},{1,9},{2,10},{3,11},{4,12},{5,13},{6,14},{7,15},{8,0},{9,1},... | collective-permute-start | bytes 393224 | tf_op jit(solution)/shard_map/ppermute | solution.py:107
